TPU v7x, 32 devices: a whole 2x2x4 slice. The times are simulated.
32 devices in a mesh: rows: 16 (over z, y, x), cols: 2 (over core).
Axes of the slice: x: 2, y: 2, z: 4, core: 2. Of those that a mesh axis runs over, the one named last changes fastest.
Arguments:
- panel: float32 [2048, 32768], P('rows', 'cols'), may hold values from -0.03125 to 0.03125
- solved: float32 [32768, 64], P('cols'), may hold values from -6 to 6
- sketch: float32 [2048, 64], P('rows'), may hold values from -6 to 6
- inverses: float32 [2, 1024, 1024], P(None, 'rows', 'cols'), may hold values from -2 to 2, as said below
- coupling: float32 [1024, 1024], P('rows', 'cols'), may hold values from -0.1875 to 0.1875
- design: bfloat16 [32768, 2048], P('rows', 'cols'), may hold values from -0.125 to 0.125
- prior: float32 [32768, 64], P(('rows', 'cols')), may hold values from -6 to 6
Outputs:
- block_solution: float32 [2048, 64], P('rows')
- leverage: float32 [32768], P(('rows', 'cols'))
Inputs may be any that keep to these rules, and one draw needn't show every extreme that they name: `inverses`: each of the two blocks is upper triangular with a positive diagonal.
All inputs are finite; a program needn't handle non-finite values.
Results may differ from a plain program's by a relative error of at most 0.00063.
Values sent between devices are 32-bit elements; how exact they have to be, the bound alone decides.
A program may use at most 64 MiB of HBM per device.

v0:
```python
import functools

import jax
import jax.numpy as jnp
from jax import lax
from jax.experimental import pallas as pl
from jax.experimental.pallas import tpu as pltpu
from jax.sharding import PartitionSpec as P

CHUNKS = 8
EARLY = 3
NT = (((1,), (1,)), ((), ()))


def nt(a, b, precision=None):
    return lax.dot_general(a, b, NT, precision=precision, preferred_element_type=jnp.float32)


def split(x):
    high = x.astype(jnp.bfloat16)
    low = (x - high.astype(jnp.float32)).astype(jnp.bfloat16)
    return jnp.concatenate([high, low], axis=0)


def kernel(
    n,
    panel, solved, sketch, inverses, coupling, design, prior,
    out_solution, out_leverage,
    panel_v, solved_v, sketch_v, design_v, prior_v,
    acc, part_tx, part_rx, right_tx, right_last, right_first,
    w_rx, w_split, y_tx, y_last, z_tx, z_all, s_tx, y_first,
    y_half, prod_tx, prod_rx, sol_tx, sol_rx, lev_tx, lev_rx,
    load_sem, w_send, w_recv, send_sem, pair_send, recv_sem,
):
    r = lax.axis_index("rows")
    c = lax.axis_index("cols")
    peer = 1 - c
    q = n // 4
    plane, p = r // q, r % q
    bottom, upper = plane // 2, plane % 2
    depth = panel.shape[1]
    step = depth // CHUNKS
    k, pr = sketch.shape
    ir = pr // 2
    width = inverses.shape[2]
    rows_here = prior.shape[1]

    def chunk(i):
        at = pl.ds(pl.multiple_of(i * step, step), step)
        return (
            pltpu.make_async_copy(panel.at[:, at], panel_v.at[:, at], load_sem.at[0, i]),
            pltpu.make_async_copy(solved.at[:, at], solved_v.at[:, at], load_sem.at[1, i]),
        )

    for i in range(CHUNKS):
        for copy in chunk(i):
            copy.start()
    late = [
        pltpu.make_async_copy(src, dst, load_sem.at[2, i])
        for i, (src, dst) in enumerate(((sketch, sketch_v), (prior, prior_v), (design, design_v)))
    ]

    barrier = pltpu.get_barrier_semaphore()

    def greet(to, core):
        pl.semaphore_signal(
            barrier, inc=1, device_id=(to, core), device_id_type=pl.DeviceIdType.MESH
        )

    @pl.when(c == 0)
    def _():
        greet(r, 1)

    @pl.when(c == 1)
    def _():
        def column(i, carry):
            greet(i * q + p, 0)
            return carry

        def others(i, carry):
            greet((r + 1 + i) % n, 1)
            return carry

        lax.fori_loop(0, 4, column, 0)
        lax.fori_loop(0, n - 1, others, 0)

    acc[...] = jnp.zeros_like(acc)

    def body(i, carry):
        for copy in chunk(i):
            copy.wait()
        at = pl.ds(pl.multiple_of(i * step, step), step)
        acc[...] += nt(split(solved_v[:, at]), split(panel_v[:, at]))
        return carry

    def remote(src, dst, to, core, sent, recv):
        return pltpu.make_async_remote_copy(
            src_ref=src,
            dst_ref=dst,
            send_sem=sent,
            recv_sem=recv,
            device_id=(to, core),
            device_id_type=pl.DeviceIdType.MESH,
        )

    def put(src, dst, to, core, sent, recv):
        here = jnp.logical_and(to == r, core == c)

        @pl.when(here)
        def _():
            pltpu.make_async_copy(src, dst, recv).start()

        @pl.when(jnp.logical_not(here))
        def _():
            remote(src, dst, to, core, sent, recv).start()

    def settle(src, dst, to, core, sent, recv):
        here = jnp.logical_and(to == r, core == c)

        @pl.when(jnp.logical_not(here))
        def _():
            remote(src, dst, to, core, sent, recv).wait_send()

    def arrived(ref, recv):
        pltpu.make_async_copy(ref, ref, recv).wait()

    def weights(act, which):
        src = (inverses.at[1], coupling, inverses.at[0])[which]
        rows_at = pl.ds(pl.multiple_of(ir * upper, ir), ir)

        def move(skip):
            size = width - skip
            cols_at = pl.ds(pl.multiple_of(width * c + skip, skip or width), size)
            act(
                src.at[:, skip:],
                w_rx.at[which, rows_at, cols_at],
                (1 + bottom) * q + p,
                1,
                w_send.at[which],
                w_recv.at[which, upper, c],
            )

        if which == 1:
            move(0)
        else:

            @pl.when(jnp.logical_and(c == bottom, upper == 1))
            def _():
                move(width // 2)

            @pl.when(jnp.logical_or(c > bottom, jnp.logical_and(c == bottom, upper == 0)))
            def _():
                move(0)

    def bulk():
        weights(put, 0)
        weights(put, 1)

    early = jnp.logical_or(c == 0, plane >= 2)

    def meet():
        pl.semaphore_wait(barrier, jnp.where(c == 0, 4, n))
        bulk()

    late[0].start()
    lax.fori_loop(0, EARLY, body, 0)
    pl.when(early)(meet)
    lax.fori_loop(EARLY, CHUNKS, body, 0)
    pl.when(jnp.logical_not(early))(meet)
    total = acc[...]
    part = (total[:k, :pr] + total[k:, :pr]) + (total[:k, pr:] + total[k:, pr:])

    def to_peer(src, dst, which, recv):
        return remote(src, dst, r, peer, pair_send.at[which], recv_sem.at[recv])

    part_copy = to_peer(part_tx, part_rx, 0, 3)
    prod_copies = [
        to_peer(
            prod_tx.at[:, i * rows_here : (i + 1) * rows_here],
            prod_rx.at[:, i * rows_here : (i + 1) * rows_here],
            1 + i,
            8,
        )
        for i in range(2)
    ]
    sol_copy = to_peer(sol_tx, sol_rx, 3, 9)
    lev_copy = to_peer(lev_tx, lev_rx, 4, 10)

    lane = lax.broadcasted_iota(jnp.int32, (k, pr), 1)

    def fold(a, b, odd):
        even_half = jnp.where(lane < ir, a, pltpu.roll(b, ir, 1))
        odd_half = jnp.where(lane < ir, pltpu.roll(a, ir, 1), b)
        return jnp.where(odd, odd_half, even_half)

    def natural(ref, t):
        at = (t // q) * q + (2 * t) % q
        a = ref[:, pl.ds(pl.multiple_of(at * pr, pr), pr)]
        b = ref[:, pl.ds(pl.multiple_of((at + 1) * pr, pr), pr)]
        return fold(a, b, (t % q) // (q // 2) == 1)

    def whole(ref):
        for t in range(2 * q):
            at = (t // q) * q + (2 * t) % q
            a = ref[:, at * pr : (at + 1) * pr]
            b = ref[:, (at + 1) * pr : (at + 2) * pr]
            if (t % q) // (q // 2) == 1:
                both = jnp.where(lane < ir, pltpu.roll(a, ir, 1), b)
            else:
                both = jnp.where(lane < ir, a, pltpu.roll(b, ir, 1))
            y_half[:, t * pr : (t + 1) * pr] = both.astype(jnp.bfloat16)

    def product(which):
        return nt(y_half[...], design_v[which * rows_here : (which + 1) * rows_here, :])

    def piece(h):
        return pl.ds(pl.multiple_of((h * q + p) * pr, pr), pr)

    def near(i):
        return (p + 1 + i) % q

    def spread(act, count, src, dst, where, core, phase, recv):
        def one(i, carry):
            act(src, dst, where(i), core, send_sem.at[phase, i], recv_sem.at[recv])
            return carry

        lax.fori_loop(0, count, one, 0)

    last_args = (right_tx, right_last.at[:, pl.ds(pl.multiple_of(pr * (r % (2 * q)), pr), pr)])

    def spread_last(act):
        def where(i):
            return (1 + i // q) * q + near(i)

        @pl.when(plane == 3)
        def _():
            spread(act, 2 * q, *last_args, where, 1, 0, 4)

        @pl.when(plane == 2)
        def _():
            spread(act, q, *last_args, where, 1, 0, 4)

    def spread_first(act):
        @pl.when(plane < 2)
        def _():
            for i in range(2):
                j = 2 * r + i
                to = (1 + j // (2 * q)) * q + j % q
                act(right_tx, right_first.at[(j % (2 * q)) // q], to, 1, send_sem.at[0, i], recv_sem.at[5])

    def spread_y_last(act):
        def where(i):
            s = i // q
            return jnp.where(s == 0, 3 - plane, jnp.where(s == 1, plane, 3 * s - 6)) * q + near(i)

        spread(act, n, y_tx, y_last.at[:, piece(bottom)], where, 1, 1, 6)

    def spread_z(act):
        @pl.when(plane == 2)
        def _():
            spread(act, 2 * q, z_tx, z_all.at[:, piece(1)], lambda i: (1 + i // q) * q + near(i), 1, 2, 7)

        @pl.when(plane == 1)
        def _():
            spread(act, q, z_tx, z_all.at[:, piece(0)], lambda i: q + near(i), 1, 2, 7)

    def spread_y_first(act):
        def where(i):
            return (i // q) * q + near(i)

        spread(act, n, s_tx, y_first.at[:, piece(bottom)], where, 0, 3, 11)

    def prepare(which, lo):
        size = 2 * width - lo
        x = w_rx[which, :, lo:]
        if which:
            wide = lax.broadcasted_iota(jnp.int32, (pr, pr), 1)
            blocks = []
            for base in range(0, size, width):
                for at in range(q):
                    i = base + (at // 2) * pr
                    j = i + width // 2
                    a, b = x[:, i : i + pr], x[:, j : j + pr]
                    if at % 2:
                        blocks.append(jnp.where(wide < ir, pltpu.roll(a, ir, 1), b))
                    else:
                        blocks.append(jnp.where(wide < ir, a, pltpu.roll(b, ir, 1)))
            x = jnp.concatenate(blocks, axis=1)
        w_split[which, :, lo:] = split(x)

    def ready(which, lo):
        skip = width // 2 if which != 1 else 0
        if skip:
            w_rx[which, ir:, lo : lo + skip] = jnp.zeros((ir, skip), jnp.float32)
        for core in range(lo // width, 2):
            for up in range(2):
                first = width * core + (skip if up == 1 and width * core == lo else 0)
                arrived(
                    w_rx.at[which, ir * up : ir * up + ir, first : width * core + width],
                    w_recv.at[which, up, core],
                )
        prepare(which, lo)

    def times(ref, which, lo):
        terms = nt(split(ref[:, lo:]), w_split[which, :, lo:])
        terms = terms[:k] + terms[k:]
        return terms[:, :pr] + terms[:, pr:]

    @pl.when(c == 0)
    def _():
        part_tx[...] = part
        part_copy.start()
        weights(put, 2)
        late[1].start()
        late[2].start()
        late[0].wait()
        late[1].wait()
        late[2].wait()
        arrived(prod_rx, recv_sem.at[8])
        prod_tx[:, :rows_here] = prod_rx[:, :rows_here] + prior_v[...]
        arrived(y_first, recv_sem.at[11])
        whole(y_first)
        theirs = product(1) + prod_rx[:, rows_here:]
        lev_tx[...] = jnp.mean(theirs * theirs, axis=0, keepdims=True)
        lev_copy.start()

        @pl.when(plane < 2)
        def _():
            mine = natural(y_first, r % (2 * q))
            sol_tx[...] = mine
            sol_copy.start()
            out_solution[...] = mine

        ours = product(0) + prod_tx[:, :rows_here]
        out_leverage[...] = jnp.mean(ours * ours, axis=0, keepdims=True)

        @pl.when(plane >= 2)
        def _():
            arrived(sol_rx, recv_sem.at[9])
            out_solution[...] = sol_rx[...]

        @pl.when(plane < 2)
        def _():
            sol_copy.wait_send()

        part_copy.wait_send()
        lev_copy.wait_send()

    @pl.when(c == 1)
    def _():
        late[0].wait()
        own = sketch_v[...] - part
        arrived(part_rx, recv_sem.at[3])
        right_tx[...] = own - part_rx[...]
        spread_last(put)
        spread_first(put)
        weights(put, 2)
        late[1].start()
        late[2].start()

        def solve(lo):
            ready(0, lo)
            arrived(right_last.at[:, lo:], recv_sem.at[4])
            y_tx[...] = times(right_last, 0, lo)
            arrived(right_first, recv_sem.at[5])
            spread_y_last(put)
            z_tx[...] = fold(right_first[0], right_first[1], p % 2 == 1)
            ready(1, 0)
            arrived(y_last, recv_sem.at[6])
            z_tx[...] = z_tx[...] - times(y_last, 1, 0)
            spread_z(put)
            ready(2, lo)
            arrived(z_all.at[:, lo:], recv_sem.at[7])
            s_tx[...] = times(z_all, 2, lo)
            spread_y_first(put)

        @pl.when(plane == 1)
        def _():
            solve(0)

        @pl.when(plane == 2)
        def _():
            solve(width)

        inner = jnp.logical_or(plane == 1, plane == 2)

        @pl.when(jnp.logical_not(inner))
        def _():
            arrived(y_last, recv_sem.at[6])

        late[1].wait()
        late[2].wait()
        whole(y_last)
        prod_tx[:, :rows_here] = product(0)
        prod_copies[0].start()
        prod_tx[:, rows_here:] = product(1) + prior_v[...]
        prod_copies[1].start()

        @pl.when(plane >= 2)
        def _():
            mine = natural(y_last, r % (2 * q))
            sol_tx[...] = mine
            sol_copy.start()
            out_solution[...] = mine

        spread_last(settle)
        spread_first(settle)

        @pl.when(inner)
        def _():
            spread_y_last(settle)
            spread_z(settle)
            spread_y_first(settle)

        for copy in prod_copies:
            copy.wait_send()

        @pl.when(plane >= 2)
        def _():
            sol_copy.wait_send()

        @pl.when(plane < 2)
        def _():
            arrived(sol_rx, recv_sem.at[9])
            out_solution[...] = sol_rx[...]

        arrived(lev_rx, recv_sem.at[10])
        out_leverage[...] = lev_rx[...]

    for which in range(3):
        weights(settle, which)


def pinned(x):
    return pltpu.with_memory_space_constraint(x, pltpu.HBM)


def fused(n, panel, solved, sketch, inverses, coupling, design, prior):
    k = sketch.shape[1]
    pr, depth = panel.shape
    rows_here = prior.shape[0]
    width = inverses.shape[2]
    f32 = jnp.float32
    out_solution, out_leverage = pl.pallas_call(
        functools.partial(kernel, n),
        out_shape=(
            jax.ShapeDtypeStruct((k, pr), f32),
            jax.ShapeDtypeStruct((1, rows_here), f32),
        ),
        in_specs=[pl.BlockSpec(memory_space=pltpu.HBM)] * 7,
        out_specs=[pl.BlockSpec(memory_space=pltpu.VMEM)] * 2,
        scratch_shapes=[
            pltpu.VMEM((pr, depth), f32),
            pltpu.VMEM((k, depth), f32),
            pltpu.VMEM((k, pr), f32),
            pltpu.VMEM(design.shape, design.dtype),
            pltpu.VMEM((k, rows_here), f32),
            pltpu.VMEM((2 * k, 2 * pr), f32),
            pltpu.VMEM((k, pr), f32),
            pltpu.VMEM((k, pr), f32),
            pltpu.VMEM((k, pr), f32),
            pltpu.VMEM((k, 2 * width), f32),
            pltpu.VMEM((2, k, pr), f32),
            pltpu.VMEM((3, pr, 2 * width), f32),
            pltpu.VMEM((3, 2 * pr, 2 * width), jnp.bfloat16),
            pltpu.VMEM((k, pr), f32),
            pltpu.VMEM((k, 2 * width), f32),
            pltpu.VMEM((k, pr), f32),
            pltpu.VMEM((k, 2 * width), f32),
            pltpu.VMEM((k, pr), f32),
            pltpu.VMEM((k, 2 * width), f32),
            pltpu.VMEM((k, 2 * width), jnp.bfloat16),
            pltpu.VMEM((k, 2 * rows_here), f32),
            pltpu.VMEM((k, 2 * rows_here), f32),
            pltpu.VMEM((k, pr), f32),
            pltpu.VMEM((k, pr), f32),
            pltpu.VMEM((1, rows_here), f32),
            pltpu.VMEM((1, rows_here), f32),
            pltpu.SemaphoreType.DMA((3, CHUNKS)),
            pltpu.SemaphoreType.DMA((3,)),
            pltpu.SemaphoreType.DMA((3, 2, 2)),
            pltpu.SemaphoreType.DMA((4, n)),
            pltpu.SemaphoreType.DMA((5,)),
            pltpu.SemaphoreType.DMA((12,)),
        ],
        compiler_params=pltpu.CompilerParams(
            collective_id=0, has_side_effects=True, vmem_limit_bytes=28 * 1024 * 1024
        ),
    )(*map(pinned, (panel, solved.T, sketch.T, inverses, coupling, design, prior.T)))
    return out_solution.T, out_leverage.reshape(rows_here)


def assemble(term):
    rows_here = lax.psum(term, "cols")
    return lax.all_gather(rows_here, "rows", axis=0, tiled=True)


def local(panel, solved, sketch, inverses, coupling, design, prior):
    highest = lax.Precision.HIGHEST
    partial_value = jnp.dot(panel, solved, precision=highest)
    local_right = sketch - lax.psum(partial_value, "cols")
    right = lax.all_gather(local_right, "rows", axis=0, tiled=True)
    blocks = right.shape[0] // 2
    width = inverses.shape[2]
    column = lax.axis_index("cols")
    offset = column * width

    def piece(vector):
        return lax.dynamic_slice_in_dim(vector, offset, width, 0)

    right_first = right[:blocks]
    right_last = right[blocks:]
    sketch_cols = right.shape[1]
    inverse_full = lax.all_gather(inverses[0], "cols", axis=1, tiled=True)
    coupling_full = lax.all_gather(coupling, "rows", axis=0, tiled=True)
    mixed = jnp.dot(inverse_full, coupling_full, precision=highest)
    term_last = jnp.dot(inverses[1], piece(right_last), precision=highest)
    term_first = jnp.dot(inverses[0], piece(right_first), precision=highest)
    joined = assemble(jnp.concatenate([term_last, term_first], axis=1))
    y_last = joined[:, :sketch_cols]
    partial_first = joined[:, sketch_cols:]
    correction = assemble(jnp.dot(mixed, piece(y_last), precision=highest))
    y_first = partial_first - correction
    solution = jnp.concatenate([y_first, y_last], axis=0)
    own_rows = sketch.shape[0]
    block_solution = lax.dynamic_slice_in_dim(
        solution, lax.axis_index("rows") * own_rows, own_rows, 0
    )
    design_cols = design.shape[1]
    rounded = lax.dynamic_slice_in_dim(solution, column * design_cols, design_cols, 0).astype(
        jnp.bfloat16
    )
    mine = lax.psum_scatter(
        jnp.dot(design, rounded, preferred_element_type=jnp.float32),
        "cols",
        scatter_dimension=0,
        tiled=True,
    )
    product = prior + mine
    leverage = jnp.mean(product * product, axis=1)
    return (block_solution, leverage)


def local_or_fused(rows, panel, solved, sketch, inverses, coupling, design, prior):
    args = (panel, solved, sketch, inverses, coupling, design, prior)
    pr, depth = panel.shape
    fits = pr == 128 and depth % (CHUNKS * 128) == 0 and sketch.shape[1] % 32 == 0
    return fused(rows, *args) if fits else local(*args)


def solution(mesh):
    in_specs = (
        P("rows", "cols"),
        P("cols", None),
        P("rows", None),
        P(None, "rows", "cols"),
        P("rows", "cols"),
        P("rows", "cols"),
        P(("rows", "cols"), None),
    )
    out_specs = (P("rows", None), P(("rows", "cols")))
    rows, cols = mesh.shape["rows"], mesh.shape["cols"]
    step = local
    if cols == 2 and rows % 8 == 0:
        step = functools.partial(local_or_fused, rows)
    return jax.shard_map(step, mesh=mesh, in_specs=in_specs, out_specs=out_specs, check_vma=False)
```

profile of v0, /device:TPU:0, one launch (start us, length us, event | category | flops | bytes accessed | tf_op | source)
XLA Modules:
  0.0 32.8 jit_solution(7341076826319514932)
XLA Ops:
  0.6 30.9 %shard_map.86 = (f32[64,128]{1,0:T(8,128)S(1)}, f32[1,1024]{1,0:T(1,128)S(1)}) custom-call(f32[128,16384]{1,0:T(8,128)} %panel.1, f32[64,16384]{1,0:T(8,128)} %bitcast.7, f32[64,128]{1,0:T(8,128)} %bitcast.9, f32[2,64,512]{2,1,0:T(8,128)} %inverses.1, f32[64,512]{1,0:T(8,128)} %coupling.1, bf16[2048,1024]{1,0:T(8,128)(2,1)} %design.1, f32[64,1024]{1,0:T(8,128)} %bitcast.8), custom_call_target="tpu_custom_call" | custom-call | tf_op jit(solution)/shard_map/pallas_call | solution.py:444
  31.6 0.6 %copy.11 = f32[128,64]{0,1:T(8,128)} copy(f32[128,64]{0,1:T(8,128)S(1)} %bitcast.5) | data formatting | bytes 65536
  32.2 0.6 %copy.12 = f32[1024]{0:T(1024)} copy(f32[1024]{0:T(1024)S(1)} %bitcast.6) | data formatting | bytes 8192
where the time goes:
time: 32.9 us; the launch traced here: 32.8 us
  Pallas kernels  30.9 us (94%)
  local copies, waits for them, and re-layouts  1.21 us (4%)
  between operations  0.64 us (2%)
    pallas_call x1, Pallas kernels, fused(): pl.pallas_call(functools.partial(kernel, n), out_shape=(jax.ShapeDtypeStr...  30.9 us
    unnamed x2, local copies, waits for them, and re-layouts  1.21 us

commit v1 on v0

--- a/solution.py
+++ b/solution.py
@@ -9,6 +9,8 @@
 
 CHUNKS = 8
 EARLY = 3
+PARTS = 1
+SLABS = 4
 NT = (((1,), (1,)), ((), ()))
 
 
@@ -29,8 +31,8 @@
     panel_v, solved_v, sketch_v, design_v, prior_v,
     acc, part_tx, part_rx, right_tx, right_last, right_first,
     w_rx, w_split, y_tx, y_last, z_tx, z_all, s_tx, y_first,
-    y_half, prod_tx, prod_rx, sol_tx, sol_rx, lev_tx, lev_rx,
-    load_sem, w_send, w_recv, send_sem, pair_send, recv_sem,
+    y_half, prod_tx, prod_rx, held, sol_tx, sol_rx, wide, design_own,
+    load_sem, w_send, w_recv, send_sem, pair_send, recv_sem, wide_send, wide_recv,
 ):
     r = lax.axis_index("rows")
     c = lax.axis_index("cols")
@@ -42,6 +44,7 @@
     step = depth // CHUNKS
     k, pr = sketch.shape
     ir = pr // 2
+    kh = k // PARTS
     width = inverses.shape[2]
     rows_here = prior.shape[1]
 
@@ -168,23 +171,24 @@
     lax.fori_loop(EARLY, CHUNKS, body, 0)
     pl.when(jnp.logical_not(early))(meet)
     total = acc[...]
-    part = (total[:k, :pr] + total[k:, :pr]) + (total[:k, pr:] + total[k:, pr:])
+    share = (total[:k, :pr] + total[k:, :pr]) + (total[:k, pr:] + total[k:, pr:])
 
     def to_peer(src, dst, which, recv):
-        return remote(src, dst, r, peer, pair_send.at[which], recv_sem.at[recv])
+        return remote(src, dst, r, peer, pair_send.at[which], recv_sem.at[recv, 0])
 
     part_copy = to_peer(part_tx, part_rx, 0, 3)
-    prod_copies = [
-        to_peer(
-            prod_tx.at[:, i * rows_here : (i + 1) * rows_here],
-            prod_rx.at[:, i * rows_here : (i + 1) * rows_here],
-            1 + i,
-            8,
-        )
-        for i in range(2)
-    ]
-    sol_copy = to_peer(sol_tx, sol_rx, 3, 9)
-    lev_copy = to_peer(lev_tx, lev_rx, 4, 10)
+    prod_copy = to_peer(prod_tx, prod_rx, 1, 0)
+    sol_copy = to_peer(sol_tx, sol_rx, 2, 1)
+
+    def group(g):
+        return slice(g * width, (g + 1) * width)
+
+    passes = [to_peer(y_first.at[:, group(g)], y_first.at[:, group(g)], 3 + g, 9 + g) for g in range(2)]
+    slab = rows_here // SLABS
+
+    def widen(i):
+        at = pl.ds(pl.multiple_of(slab * i, slab), slab)
+        return remote(wide.at[at], wide.at[at], r, 1, wide_send.at[i], wide_recv.at[i])
 
     lane = lax.broadcasted_iota(jnp.int32, (k, pr), 1)
 
@@ -199,9 +203,9 @@
         b = ref[:, pl.ds(pl.multiple_of((at + 1) * pr, pr), pr)]
         return fold(a, b, (t % q) // (q // 2) == 1)
 
-    def whole(ref):
-        for t in range(2 * q):
-            at = (t // q) * q + (2 * t) % q
+    def round_group(ref, g):
+        for t in range(g * q, (g + 1) * q):
+            at = g * q + (2 * t) % q
             a = ref[:, at * pr : (at + 1) * pr]
             b = ref[:, (at + 1) * pr : (at + 2) * pr]
             if (t % q) // (q // 2) == 1:
@@ -213,32 +217,54 @@
     def product(which):
         return nt(y_half[...], design_v[which * rows_here : (which + 1) * rows_here, :])
 
+    def finish(g, weights_of):
+        round_group(y_first, g)
+        held[...] += nt(y_half[:, group(g)], weights_of[:rows_here, group(g)])
+
+    def conclude():
+        total_here = held[...]
+        out_leverage[...] = jnp.mean(total_here * total_here, axis=0, keepdims=True)
+
+        @pl.when(plane < 2)
+        def _():
+            out_solution[...] = natural(y_first, r % (2 * q))
+
     def piece(h):
         return pl.ds(pl.multiple_of((h * q + p) * pr, pr), pr)
 
     def near(i):
         return (p + 1 + i) % q
 
-    def spread(act, count, src, dst, where, core, phase, recv):
+    def mixed(i, count):
+        planes = count // q
+        return (1 + i % planes) * q + near(i // planes)
+
+    def spread(act, span, src, dst, cols_at, where, core, phase, part):
+        rows_at = slice(part * kh, (part + 1) * kh)
+
         def one(i, carry):
-            act(src, dst, where(i), core, send_sem.at[phase, i], recv_sem.at[recv])
+            to = where(i // q) * q + near(i) if phase else mixed(i, span[1])
+            sent = send_sem.at[phase, part, i]
+            recv = recv_sem.at[4 + phase if phase < 3 else 7 + bottom, part]
+            act(src.at[rows_at], dst.at[rows_at, cols_at], to, core, sent, recv)
             return carry
 
-        lax.fori_loop(0, count, one, 0)
-
-    last_args = (right_tx, right_last.at[:, pl.ds(pl.multiple_of(pr * (r % (2 * q)), pr), pr)])
+        lax.fori_loop(*span, one, 0)
+
+    last_at = pl.ds(pl.multiple_of(pr * (r % (2 * q)), pr), pr)
 
     def spread_last(act):
-        def where(i):
-            return (1 + i // q) * q + near(i)
+        def send(planes):
+            for part in range(PARTS):
+                spread(act, (0, planes * q), right_tx, right_last, last_at, lambda s: 1 + s, 1, 0, part)
 
         @pl.when(plane == 3)
         def _():
-            spread(act, 2 * q, *last_args, where, 1, 0, 4)
+            send(2)
 
         @pl.when(plane == 2)
         def _():
-            spread(act, q, *last_args, where, 1, 0, 4)
+            send(1)
 
     def spread_first(act):
         @pl.when(plane < 2)
@@ -246,29 +272,28 @@
             for i in range(2):
                 j = 2 * r + i
                 to = (1 + j // (2 * q)) * q + j % q
-                act(right_tx, right_first.at[(j % (2 * q)) // q], to, 1, send_sem.at[0, i], recv_sem.at[5])
-
-    def spread_y_last(act):
-        def where(i):
-            s = i // q
-            return jnp.where(s == 0, 3 - plane, jnp.where(s == 1, plane, 3 * s - 6)) * q + near(i)
-
-        spread(act, n, y_tx, y_last.at[:, piece(bottom)], where, 1, 1, 6)
-
-    def spread_z(act):
+                act(right_tx, right_first.at[(j % (2 * q)) // q], to, 1, send_sem.at[0, 0, i], recv_sem.at[2, 0])
+
+    def spread_y_last(act, part, span):
+        def where(s):
+            return jnp.where(s == 0, 3 - plane, jnp.where(s == 1, plane, 3 * s - 6))
+
+        spread(act, span, y_tx, y_last, piece(bottom), where, 1, 1, part)
+
+    def spread_z(act, part):
         @pl.when(plane == 2)
         def _():
-            spread(act, 2 * q, z_tx, z_all.at[:, piece(1)], lambda i: (1 + i // q) * q + near(i), 1, 2, 7)
+            spread(act, (0, 2 * q), z_tx, z_all, piece(1), lambda s: 1 + s, 1, 2, part)
 
         @pl.when(plane == 1)
         def _():
-            spread(act, q, z_tx, z_all.at[:, piece(0)], lambda i: q + near(i), 1, 2, 7)
-
-    def spread_y_first(act):
-        def where(i):
-            return (i // q) * q + near(i)
-
-        spread(act, n, s_tx, y_first.at[:, piece(bottom)], where, 0, 3, 11)
+            spread(act, (0, q), z_tx, z_all, piece(0), lambda s: 1 + s, 1, 2, part)
+
+    def spread_y_first(act, part):
+        spread(act, (0, n), s_tx, y_first, piece(bottom), lambda s: s, 1, 3, part)
+
+    def here(ref, phase, part, lo=0):
+        arrived(ref.at[part * kh : (part + 1) * kh, lo:], recv_sem.at[4 + phase, part])
 
     def prepare(which, lo):
         size = 2 * width - lo
@@ -301,14 +326,14 @@
                 )
         prepare(which, lo)
 
-    def times(ref, which, lo):
-        terms = nt(split(ref[:, lo:]), w_split[which, :, lo:])
-        terms = terms[:k] + terms[k:]
+    def times(ref, which, part, lo):
+        terms = nt(split(ref[part * kh : (part + 1) * kh, lo:]), w_split[which, :, lo:])
+        terms = terms[:kh] + terms[kh:]
         return terms[:, :pr] + terms[:, pr:]
 
     @pl.when(c == 0)
     def _():
-        part_tx[...] = part
+        part_tx[...] = share
         part_copy.start()
         weights(put, 2)
         late[1].start()
@@ -316,41 +341,40 @@
         late[0].wait()
         late[1].wait()
         late[2].wait()
-        arrived(prod_rx, recv_sem.at[8])
-        prod_tx[:, :rows_here] = prod_rx[:, :rows_here] + prior_v[...]
-        arrived(y_first, recv_sem.at[11])
-        whole(y_first)
-        theirs = product(1) + prod_rx[:, rows_here:]
-        lev_tx[...] = jnp.mean(theirs * theirs, axis=0, keepdims=True)
-        lev_copy.start()
-
-        @pl.when(plane < 2)
-        def _():
-            mine = natural(y_first, r % (2 * q))
-            sol_tx[...] = mine
-            sol_copy.start()
-            out_solution[...] = mine
-
-        ours = product(0) + prod_tx[:, :rows_here]
-        out_leverage[...] = jnp.mean(ours * ours, axis=0, keepdims=True)
+
+        def share_slab(i, carry):
+            at = pl.ds(pl.multiple_of(slab * i, slab), slab)
+            theirs = pl.ds(pl.multiple_of(rows_here + slab * i, slab), slab)
+            wide[at, :] = design_v[theirs, :].astype(jnp.float32)
+            widen(i).start()
+            return carry
+
+        lax.fori_loop(0, SLABS, share_slab, 0)
+        arrived(prod_rx, recv_sem.at[0, 0])
+        held[...] = prod_rx[...] + prior_v[...]
 
         @pl.when(plane >= 2)
         def _():
-            arrived(sol_rx, recv_sem.at[9])
+            arrived(sol_rx, recv_sem.at[1, 0])
             out_solution[...] = sol_rx[...]
 
-        @pl.when(plane < 2)
-        def _():
-            sol_copy.wait_send()
-
+        for g in (1, 0):
+            arrived(y_first.at[:, group(g)], recv_sem.at[9 + g, 0])
+            finish(g, design_v)
+        conclude()
         part_copy.wait_send()
-        lev_copy.wait_send()
+
+        def sent_slab(i, carry):
+            widen(i).wait_send()
+            return carry
+
+        lax.fori_loop(0, SLABS, sent_slab, 0)
 
     @pl.when(c == 1)
     def _():
         late[0].wait()
-        own = sketch_v[...] - part
-        arrived(part_rx, recv_sem.at[3])
+        own = sketch_v[...] - share
+        arrived(part_rx, recv_sem.at[3, 0])
         right_tx[...] = own - part_rx[...]
         spread_last(put)
         spread_first(put)
@@ -360,19 +384,25 @@
 
         def solve(lo):
             ready(0, lo)
-            arrived(right_last.at[:, lo:], recv_sem.at[4])
-            y_tx[...] = times(right_last, 0, lo)
-            arrived(right_first, recv_sem.at[5])
-            spread_y_last(put)
+            for part in range(PARTS):
+                here(right_last, 0, part, lo)
+                y_tx[part * kh : (part + 1) * kh] = times(right_last, 0, part, lo)
+                spread_y_last(put, part, (0, 2 * q))
+            for part in range(PARTS):
+                spread_y_last(put, part, (2 * q, n))
+            ready(1, 0)
+            arrived(right_first, recv_sem.at[2, 0])
             z_tx[...] = fold(right_first[0], right_first[1], p % 2 == 1)
-            ready(1, 0)
-            arrived(y_last, recv_sem.at[6])
-            z_tx[...] = z_tx[...] - times(y_last, 1, 0)
-            spread_z(put)
+            for part in range(PARTS):
+                at = slice(part * kh, (part + 1) * kh)
+                here(y_last, 1, part)
+                z_tx[at] = z_tx[at] - times(y_last, 1, part, 0)
+                spread_z(put, part)
             ready(2, lo)
-            arrived(z_all.at[:, lo:], recv_sem.at[7])
-            s_tx[...] = times(z_all, 2, lo)
-            spread_y_first(put)
+            for part in range(PARTS):
+                here(z_all, 2, part, lo)
+                s_tx[part * kh : (part + 1) * kh] = times(z_all, 2, part, lo)
+                spread_y_first(put, part)
 
         @pl.when(plane == 1)
         def _():
@@ -386,15 +416,16 @@
 
         @pl.when(jnp.logical_not(inner))
         def _():
-            arrived(y_last, recv_sem.at[6])
+            for part in range(PARTS):
+                here(y_last, 1, part)
 
         late[1].wait()
         late[2].wait()
-        whole(y_last)
-        prod_tx[:, :rows_here] = product(0)
-        prod_copies[0].start()
-        prod_tx[:, rows_here:] = product(1) + prior_v[...]
-        prod_copies[1].start()
+        for g in range(2):
+            round_group(y_last, g)
+        prod_tx[...] = product(0)
+        prod_copy.start()
+        held[...] = product(1) + prior_v[...]
 
         @pl.when(plane >= 2)
         def _():
@@ -403,32 +434,50 @@
             sol_copy.start()
             out_solution[...] = mine
 
+        def narrow_slab(i, carry):
+            at = pl.ds(pl.multiple_of(slab * i, slab), slab)
+            arrived(wide.at[at], wide_recv.at[i])
+            design_own[at, :] = wide[at, :].astype(jnp.bfloat16)
+            return carry
+
+        lax.fori_loop(0, SLABS, narrow_slab, 0)
+        for g in (1, 0):
+            arrived(y_first.at[:, group(g)], recv_sem.at[7 + g, 0])
+            passes[g].start()
+        for g in (1, 0):
+            finish(g, design_own)
+        conclude()
         spread_last(settle)
         spread_first(settle)
 
         @pl.when(inner)
         def _():
-            spread_y_last(settle)
-            spread_z(settle)
-            spread_y_first(settle)
-
-        for copy in prod_copies:
+            for part in range(PARTS):
+                spread_y_last(settle, part, (0, n))
+                spread_z(settle, part)
+                spread_y_first(settle, part)
+
+        prod_copy.wait_send()
+        for copy in passes:
             copy.wait_send()
 
         @pl.when(plane >= 2)
         def _():
             sol_copy.wait_send()
-
-        @pl.when(plane < 2)
-        def _():
-            arrived(sol_rx, recv_sem.at[9])
-            out_solution[...] = sol_rx[...]
-
-        arrived(lev_rx, recv_sem.at[10])
-        out_leverage[...] = lev_rx[...]
 
     for which in range(3):
         weights(settle, which)
+
+
+def emit(solution_v, leverage_v, out_solution, out_leverage, sem):
+    copies = [
+        pltpu.make_async_copy(solution_v, out_solution, sem.at[0]),
+        pltpu.make_async_copy(leverage_v, out_leverage, sem.at[1]),
+    ]
+    for copy in copies:
+        copy.start()
+    for copy in copies:
+        copy.wait()
 
 
 def pinned(x):
@@ -470,23 +519,36 @@
             pltpu.VMEM((k, pr), f32),
             pltpu.VMEM((k, 2 * width), f32),
             pltpu.VMEM((k, 2 * width), jnp.bfloat16),
-            pltpu.VMEM((k, 2 * rows_here), f32),
-            pltpu.VMEM((k, 2 * rows_here), f32),
-            pltpu.VMEM((k, pr), f32),
-            pltpu.VMEM((k, pr), f32),
-            pltpu.VMEM((1, rows_here), f32),
-            pltpu.VMEM((1, rows_here), f32),
+            pltpu.VMEM((k, rows_here), f32),
+            pltpu.VMEM((k, rows_here), f32),
+            pltpu.VMEM((k, rows_here), f32),
+            pltpu.VMEM((k, pr), f32),
+            pltpu.VMEM((k, pr), f32),
+            pltpu.VMEM((rows_here, design.shape[1]), f32),
+            pltpu.VMEM((rows_here, design.shape[1]), design.dtype),
             pltpu.SemaphoreType.DMA((3, CHUNKS)),
             pltpu.SemaphoreType.DMA((3,)),
             pltpu.SemaphoreType.DMA((3, 2, 2)),
-            pltpu.SemaphoreType.DMA((4, n)),
+            pltpu.SemaphoreType.DMA((4, PARTS, n)),
             pltpu.SemaphoreType.DMA((5,)),
-            pltpu.SemaphoreType.DMA((12,)),
+            pltpu.SemaphoreType.DMA((11, PARTS)),
+            pltpu.SemaphoreType.DMA((SLABS,)),
+            pltpu.SemaphoreType.DMA((SLABS,)),
         ],
         compiler_params=pltpu.CompilerParams(
-            collective_id=0, has_side_effects=True, vmem_limit_bytes=28 * 1024 * 1024
+            collective_id=0, has_side_effects=True, vmem_limit_bytes=36 * 1024 * 1024
         ),
     )(*map(pinned, (panel, solved.T, sketch.T, inverses, coupling, design, prior.T)))
+    out_solution, out_leverage = pl.pallas_call(
+        emit,
+        out_shape=(
+            jax.ShapeDtypeStruct((k, pr), f32),
+            jax.ShapeDtypeStruct((1, rows_here), f32),
+        ),
+        in_specs=[pl.BlockSpec(memory_space=pltpu.VMEM)] * 2,
+        out_specs=[pl.BlockSpec(memory_space=pltpu.HBM)] * 2,
+        scratch_shapes=[pltpu.SemaphoreType.DMA((2,))],
+    )(*(pltpu.with_memory_space_constraint(x, pltpu.VMEM) for x in (out_solution, out_leverage)))
     return out_solution.T, out_leverage.reshape(rows_here)
 
 

time: 32.9 us -> 31.5 us (0.957)
  local copies, waits for them, and re-layouts: 1.21 us -> 0 us
    unnamed x2 -> x0, local copies, waits for them, and re-layouts: 1.21 us -> none
    pallas_call x1, Pallas kernels: 30.9 us -> 30 us  [fused(): pl.pallas_call(functools.partial(kernel, n), out_shape=(jax.ShapeDtypeStr...]
    pallas_call x0 -> x1, Pallas kernels: none -> 0.64 us  [fused(): pl.pallas_call(emit, out_shape=(jax.ShapeDtypeStruct((k, pr), f32), jax.S...]
where the time goes in v1:
time: 31.5 us; the launch traced here: 31.3 us
  Pallas kernels  30.7 us (97%)
  between operations  0.64 us (2%)
    pallas_call x1, Pallas kernels, fused(): pl.pallas_call(functools.partial(kernel, n), out_shape=(jax.ShapeDtypeStr...  30 us
    pallas_call x1, Pallas kernels, fused(): pl.pallas_call(emit, out_shape=(jax.ShapeDtypeStruct((k, pr), f32), jax.S...  0.64 us

profile of v1, /device:TPU:0, one launch (start us, length us, event | category | flops | bytes accessed | tf_op | source)
XLA Modules:
  0.0 31.3 jit_solution(16824606454674144358)
XLA Ops:
  0.6 30.0 %shard_map.86 = (f32[64,128]{1,0:T(8,128)S(1)}, f32[1,1024]{1,0:T(1,128)S(1)}) custom-call(f32[128,16384]{1,0:T(8,128)} %panel.1, f32[64,16384]{1,0:T(8,128)} %bitcast.5, f32[64,128]{1,0:T(8,128)} %bitcast.7, f32[2,64,512]{2,1,0:T(8,128)} %inverses.1, f32[64,512]{1,0:T(8,128)} %coupling.1, bf16[2048,1024]{1,0:T(8,128)(2,1)} %design.1, f32[64,1024]{1,0:T(8,128)} %bitcast.6), custom_call_target="tpu_custom_call" | custom-call | tf_op jit(solution)/shard_map/pallas_call | solution.py:493
  30.7 0.6 %shard_map.87 = (f32[64,128]{1,0:T(8,128)}, f32[1,1024]{1,0:T(1,128)}) custom-call(f32[64,128]{1,0:T(8,128)S(1)} %get-tuple-element.6.solution_v, f32[1,1024]{1,0:T(1,128)S(1)} %get-tuple-element.7.leverage_v), custom_call_target="tpu_custom_call" | custom-call | tf_op jit(solution)/shard_map/pallas_call | solution.py:542

commit v2 on v1

--- a/solution.py
+++ b/solution.py
@@ -8,7 +8,7 @@
 from jax.sharding import PartitionSpec as P
 
 CHUNKS = 8
-EARLY = 3
+EARLY = 4
 PARTS = 1
 SLABS = 4
 NT = (((1,), (1,)), ((), ()))
@@ -74,6 +74,14 @@
     def _():
         greet(r, 1)
 
+        @pl.when(r == 0)
+        def _():
+            def solvers(i, carry):
+                greet(q + i, 1)
+                return carry
+
+            lax.fori_loop(0, 2 * q, solvers, 0)
+
     @pl.when(c == 1)
     def _():
         def column(i, carry):
@@ -160,14 +168,16 @@
         weights(put, 1)
 
     early = jnp.logical_or(c == 0, plane >= 2)
+    inner = jnp.logical_or(plane == 1, plane == 2)
 
     def meet():
-        pl.semaphore_wait(barrier, jnp.where(c == 0, 4, n))
+        pl.semaphore_wait(barrier, jnp.where(c == 0, 4, jnp.where(inner, n + 1, n)))
         bulk()
 
     late[0].start()
+    pl.when(plane == 3)(meet)
     lax.fori_loop(0, EARLY, body, 0)
-    pl.when(early)(meet)
+    pl.when(jnp.logical_and(early, plane < 3))(meet)
     lax.fori_loop(EARLY, CHUNKS, body, 0)
     pl.when(jnp.logical_not(early))(meet)
     total = acc[...]
@@ -243,7 +253,7 @@
         rows_at = slice(part * kh, (part + 1) * kh)
 
         def one(i, carry):
-            to = where(i // q) * q + near(i) if phase else mixed(i, span[1])
+            to = (mixed(i, span[1]), where(i // q) * q + near(i), where(i // q) * q + near(i), i)[phase]
             sent = send_sem.at[phase, part, i]
             recv = recv_sem.at[4 + phase if phase < 3 else 7 + bottom, part]
             act(src.at[rows_at], dst.at[rows_at, cols_at], to, core, sent, recv)
@@ -290,7 +300,9 @@
             spread(act, (0, q), z_tx, z_all, piece(0), lambda s: 1 + s, 1, 2, part)
 
     def spread_y_first(act, part):
-        spread(act, (0, n), s_tx, y_first, piece(bottom), lambda s: s, 1, 3, part)
+        at = piece(bottom)
+        act(s_tx, y_first.at[:, at], 0, 0, pair_send.at[5], recv_sem.at[9 + bottom, 0])
+        spread(act, (0, n), s_tx, y_first, at, lambda s: s, 1, 3, part)
 
     def here(ref, phase, part, lo=0):
         arrived(ref.at[part * kh : (part + 1) * kh, lo:], recv_sem.at[4 + phase, part])
@@ -412,8 +424,6 @@
         def _():
             solve(width)
 
-        inner = jnp.logical_or(plane == 1, plane == 2)
-
         @pl.when(jnp.logical_not(inner))
         def _():
             for part in range(PARTS):
@@ -443,7 +453,7 @@
         lax.fori_loop(0, SLABS, narrow_slab, 0)
         for g in (1, 0):
             arrived(y_first.at[:, group(g)], recv_sem.at[7 + g, 0])
-            passes[g].start()
+            pl.when(r > 0)(passes[g].start)
         for g in (1, 0):
             finish(g, design_own)
         conclude()
@@ -459,7 +469,7 @@
 
         prod_copy.wait_send()
         for copy in passes:
-            copy.wait_send()
+            pl.when(r > 0)(copy.wait_send)
 
         @pl.when(plane >= 2)
         def _():
@@ -530,7 +540,7 @@
             pltpu.SemaphoreType.DMA((3,)),
             pltpu.SemaphoreType.DMA((3, 2, 2)),
             pltpu.SemaphoreType.DMA((4, PARTS, n)),
-            pltpu.SemaphoreType.DMA((5,)),
+            pltpu.SemaphoreType.DMA((6,)),
             pltpu.SemaphoreType.DMA((11, PARTS)),
             pltpu.SemaphoreType.DMA((SLABS,)),
             pltpu.SemaphoreType.DMA((SLABS,)),

time: 31.5 us -> 30.9 us (0.981)
  Pallas kernels: 30.7 us -> 30.1 us
    pallas_call x1, Pallas kernels: 30 us -> 29.5 us  [fused(): pl.pallas_call(functools.partial(kernel, n), out_shape=(jax.ShapeDtypeStr...]
where the time goes in v2:
time: 30.9 us; the launch traced here: 30.7 us
  Pallas kernels  30.1 us (97%)
  between operations  0.64 us (2%)
    pallas_call x1, Pallas kernels, fused(): pl.pallas_call(functools.partial(kernel, n), out_shape=(jax.ShapeDtypeStr...  29.5 us
    pallas_call x1, Pallas kernels, fused(): pl.pallas_call(emit, out_shape=(jax.ShapeDtypeStruct((k, pr), f32), jax.S...  0.64 us

profile of v2, /device:TPU:0, one launch (start us, length us, event | category | flops | bytes accessed | tf_op | source)
XLA Modules:
  0.0 30.7 jit_solution(15962755084028831160)
XLA Ops:
  0.6 29.5 %shard_map.86 = (f32[64,128]{1,0:T(8,128)S(1)}, f32[1,1024]{1,0:T(1,128)S(1)}) custom-call(f32[128,16384]{1,0:T(8,128)} %panel.1, f32[64,16384]{1,0:T(8,128)} %bitcast.5, f32[64,128]{1,0:T(8,128)} %bitcast.7, f32[2,64,512]{2,1,0:T(8,128)} %inverses.1, f32[64,512]{1,0:T(8,128)} %coupling.1, bf16[2048,1024]{1,0:T(8,128)(2,1)} %design.1, f32[64,1024]{1,0:T(8,128)} %bitcast.6), custom_call_target="tpu_custom_call" | custom-call | tf_op jit(solution)/shard_map/pallas_call | solution.py:503
  30.1 0.6 %shard_map.87 = (f32[64,128]{1,0:T(8,128)}, f32[1,1024]{1,0:T(1,128)}) custom-call(f32[64,128]{1,0:T(8,128)S(1)} %get-tuple-element.6.solution_v, f32[1,1024]{1,0:T(1,128)S(1)} %get-tuple-element.7.leverage_v), custom_call_target="tpu_custom_call" | custom-call | tf_op jit(solution)/shard_map/pallas_call | solution.py:552

commit v3 on v2

--- a/solution.py
+++ b/solution.py
@@ -7,9 +7,10 @@
 from jax.experimental.pallas import tpu as pltpu
 from jax.sharding import PartitionSpec as P
 
-CHUNKS = 8
-EARLY = 4
+CHUNKS = 5
+EARLY = 2
 PARTS = 1
+LEAD = 16
 SLABS = 4
 NT = (((1,), (1,)), ((), ()))
 
@@ -41,21 +42,28 @@
     plane, p = r // q, r % q
     bottom, upper = plane // 2, plane % 2
     depth = panel.shape[1]
-    step = depth // CHUNKS
+    lead = depth // LEAD
+    step = (depth - lead) // CHUNKS
     k, pr = sketch.shape
     ir = pr // 2
     kh = k // PARTS
     width = inverses.shape[2]
     rows_here = prior.shape[1]
 
+    def span_of(i):
+        if i is None:
+            return pl.ds(0, lead)
+        return pl.ds(pl.multiple_of(lead + i * step, 128), step)
+
     def chunk(i):
-        at = pl.ds(pl.multiple_of(i * step, step), step)
+        at = span_of(i)
+        i = CHUNKS if i is None else i
         return (
             pltpu.make_async_copy(panel.at[:, at], panel_v.at[:, at], load_sem.at[0, i]),
             pltpu.make_async_copy(solved.at[:, at], solved_v.at[:, at], load_sem.at[1, i]),
         )
 
-    for i in range(CHUNKS):
+    for i in (None, *range(CHUNKS)):
         for copy in chunk(i):
             copy.start()
     late = [
@@ -95,13 +103,15 @@
         lax.fori_loop(0, 4, column, 0)
         lax.fori_loop(0, n - 1, others, 0)
 
-    acc[...] = jnp.zeros_like(acc)
-
-    def body(i, carry):
+
+    def gathered(i):
         for copy in chunk(i):
             copy.wait()
-        at = pl.ds(pl.multiple_of(i * step, step), step)
-        acc[...] += nt(split(solved_v[:, at]), split(panel_v[:, at]))
+        at = span_of(i)
+        return nt(split(solved_v[:, at]), split(panel_v[:, at]))
+
+    def body(i, carry):
+        acc[...] += gathered(i)
         return carry
 
     def remote(src, dst, to, core, sent, recv):
@@ -176,6 +186,7 @@
 
     late[0].start()
     pl.when(plane == 3)(meet)
+    acc[...] = gathered(None)
     lax.fori_loop(0, EARLY, body, 0)
     pl.when(jnp.logical_and(early, plane < 3))(meet)
     lax.fori_loop(EARLY, CHUNKS, body, 0)
@@ -454,7 +465,6 @@
         for g in (1, 0):
             arrived(y_first.at[:, group(g)], recv_sem.at[7 + g, 0])
             pl.when(r > 0)(passes[g].start)
-        for g in (1, 0):
             finish(g, design_own)
         conclude()
         spread_last(settle)
@@ -536,7 +546,7 @@
             pltpu.VMEM((k, pr), f32),
             pltpu.VMEM((rows_here, design.shape[1]), f32),
             pltpu.VMEM((rows_here, design.shape[1]), design.dtype),
-            pltpu.SemaphoreType.DMA((3, CHUNKS)),
+            pltpu.SemaphoreType.DMA((3, CHUNKS + 1)),
             pltpu.SemaphoreType.DMA((3,)),
             pltpu.SemaphoreType.DMA((3, 2, 2)),
             pltpu.SemaphoreType.DMA((4, PARTS, n)),
@@ -616,7 +626,7 @@
 def local_or_fused(rows, panel, solved, sketch, inverses, coupling, design, prior):
     args = (panel, solved, sketch, inverses, coupling, design, prior)
     pr, depth = panel.shape
-    fits = pr == 128 and depth % (CHUNKS * 128) == 0 and sketch.shape[1] % 32 == 0
+    fits = pr == 128 and depth % (LEAD * 128) == 0 and (depth - depth // LEAD) % (CHUNKS * 128) == 0 and sketch.shape[1] % 32 == 0
     return fused(rows, *args) if fits else local(*args)
 
 

time: 30.9 us -> 30.8 us (level)
  no operation moved by 1% of the time
where the time goes in v3:
time: 30.8 us; the launch traced here: 30.7 us
  Pallas kernels  30 us (97%)
  between operations  0.64 us (2%)
    pallas_call x1, Pallas kernels, fused(): pl.pallas_call(functools.partial(kernel, n), out_shape=(jax.ShapeDtypeStr...  29.4 us
    pallas_call x1, Pallas kernels, fused(): pl.pallas_call(emit, out_shape=(jax.ShapeDtypeStruct((k, pr), f32), jax.S...  0.64 us

profile of v3, /device:TPU:0, one launch (start us, length us, event | category | flops | bytes accessed | tf_op | source)
XLA Modules:
  0.0 30.7 jit_solution(4580067785221863064)
XLA Ops:
  0.6 29.4 %shard_map.86 = (f32[64,128]{1,0:T(8,128)S(1)}, f32[1,1024]{1,0:T(1,128)S(1)}) custom-call(f32[128,16384]{1,0:T(8,128)} %panel.1, f32[64,16384]{1,0:T(8,128)} %bitcast.5, f32[64,128]{1,0:T(8,128)} %bitcast.7, f32[2,64,512]{2,1,0:T(8,128)} %inverses.1, f32[64,512]{1,0:T(8,128)} %coupling.1, bf16[2048,1024]{1,0:T(8,128)(2,1)} %design.1, f32[64,1024]{1,0:T(8,128)} %bitcast.6), custom_call_target="tpu_custom_call" | custom-call | tf_op jit(solution)/shard_map/pallas_call | solution.py:513
  30.0 0.6 %shard_map.87 = (f32[64,128]{1,0:T(8,128)}, f32[1,1024]{1,0:T(1,128)}) custom-call(f32[64,128]{1,0:T(8,128)S(1)} %get-tuple-element.6.solution_v, f32[1,1024]{1,0:T(1,128)S(1)} %get-tuple-element.7.leverage_v), custom_call_target="tpu_custom_call" | custom-call | tf_op jit(solution)/shard_map/pallas_call | solution.py:562
